TPU v7x, 256 devices: a whole 4x4x8 slice. The times are simulated.
256 devices in a mesh: seq: 2 (over core), chan: 16 (over y, x), batch: 8 (over z).
Axes of the slice: x: 4, y: 4, z: 8, core: 2. Of those that a mesh axis runs over, the one named last changes fastest.
Arguments:
- ssm_input: bfloat16 [16384, 4096], P(('batch', 'seq'), 'chan'), parts along dimension 0, may hold values from -6 to 6
- gate_z: bfloat16 [16384, 4096], P(('batch', 'seq'), 'chan'), parts along dimension 0, may hold values from -6 to 6
- proj_forward: bfloat16 [2, 16384, 128], P(None, ('batch', 'seq')), parts along dimension 1, may hold values from -2 to 2
- proj_backward: bfloat16 [2, 16384, 128], P(None, ('batch', 'seq')), parts along dimension 1, may hold values from -2 to 2
- step_raw: float32 [2, 64, 16384], P(None, 'chan', ('batch', 'seq')), parts along dimension 2, may hold values from -3 to 3
- head_params: float32 [2, 2, 64], P(None, None, 'chan'), may hold values from -4 to 1, as said below
- skip_gain: float32 [64], P('chan'), may hold values from 0.25 to 2
- norm_gain: float32 [4096], P('chan'), may hold values from 0.5 to 1.5
- out_weight: bfloat16 [4096, 2048], P(None, 'chan'), may hold values from -0.09375 to 0.09375
Outputs:
- mixed: bfloat16 [16384, 2048], P(('batch', 'seq'), 'chan'), parts along dimension 0
There are 8 independent parts, one for each index of `batch`. A program takes and returns all parts, laid end to end along the dimension named above; an argument that names none is the same for every part. Nothing has to cross between parts.
Inputs may be any that keep to these rules, and one draw needn't show every extreme that they name: `head_params`: index 0 of the second dimension holds positive decay rates, index 1 time-step biases.
All inputs are finite; a program needn't handle non-finite values.
Results may differ from a plain program's by a relative error of at most 0.0085.
Values may be sent and summed in bfloat16 or wider, within the bound.
A program may use at most 128 MiB of HBM per device.

v0:
```python
import jax
import jax.numpy as jnp
from jax import lax
from jax.sharding import PartitionSpec as P

SPAN = 256
INNER = 4096


def sent_together(arrays, axis, dim, along):
    columns = [a.reshape(*a.shape[:along], -1) for a in arrays]
    both = jnp.concatenate(columns, axis=along)
    whole, at, done = (lax.all_gather(both, axis, axis=dim, tiled=True), 0, [])
    for a, column in zip(arrays, columns):
        slab = whole[..., at : at + column.shape[along]]
        done.append(slab.reshape(*slab.shape[:along], *a.shape[along:]))
        at += column.shape[along]
    return tuple(done)


def copy_for_each(value, axis):
    copies = jnp.broadcast_to(value, (lax.axis_size(axis), *value.shape))
    return lax.all_to_all(copies, axis, split_axis=0, concat_axis=0, tiled=True)


def taken_together(value, axis):
    everything = copy_for_each(value, axis)
    return jnp.sum(everything, axis=0)


def local_scan(blocks_x, b_rows, c_rows, steps_here, decay_rates):
    cumlog = jnp.cumsum(-decay_rates[None, :, None] * steps_here, axis=2)
    scores = jnp.einsum("cqn,csn->cqs", c_rows, b_rows, preferred_element_type=jnp.float32)
    lower_mask = jnp.tril(jnp.ones((SPAN, SPAN), dtype=bool))
    log_gaps = cumlog[:, :, :, None] - cumlog[:, :, None, :]
    decays = jnp.where(lower_mask, jnp.exp(jnp.where(lower_mask, log_gaps, 0.0)), 0.0)
    weights = (scores[:, None] * decays * steps_here[:, :, None, :]).astype(jnp.bfloat16)
    intra_out = jnp.einsum("chts,cshp->cthp", weights, blocks_x, preferred_element_type=jnp.float32)
    end_logs = cumlog[:, :, -1]
    in_weights = jnp.exp(end_logs[:, :, None] - cumlog) * steps_here
    b_weighted = (b_rows[:, None].astype(jnp.float32) * in_weights[..., None]).astype(jnp.bfloat16)
    block_states = jnp.einsum(
        "cshp,chsn->chpn", blocks_x, b_weighted, preferred_element_type=jnp.float32
    )

    def advance(carried, inputs):
        gain_log, block_state = inputs
        return (jnp.exp(gain_log)[:, None, None] * carried + block_state, carried)

    initial = jnp.zeros(block_states.shape[1:], jnp.float32)
    end_state, entering = lax.scan(advance, initial, (end_logs, block_states))
    before = jnp.cumsum(end_logs, axis=0) - end_logs
    whole_decay = jnp.exp(jnp.sum(end_logs, axis=0))
    return ((intra_out, entering, cumlog, before, c_rows), (whole_decay, end_state))


def finish(pieces, carried):
    intra_out, entering, cumlog, before, c_rows = pieces
    states = entering + jnp.exp(before)[:, :, None, None] * carried[None]
    inter = jnp.einsum("ctn,chpn->cthp", c_rows.astype(jnp.float32), states)
    inter = inter * jnp.exp(cumlog).transpose(0, 2, 1)[..., None]
    outputs = intra_out + inter
    return outputs.reshape(outputs.shape[0] * outputs.shape[1], -1)


def body(
    ssm_input,
    gate_z,
    proj_forward,
    proj_backward,
    step_raw,
    head_params,
    skip_gain,
    norm_gain,
    out_weight,
):
    frames, inner_here = ssm_input.shape
    heads_here = step_raw.shape[1]
    width = inner_here // heads_here
    blocks = frames // SPAN
    shape_x = (blocks, SPAN, heads_here, width)
    shape_rows = (blocks, SPAN, proj_forward.shape[2])

    def to_blocks(steps):
        return steps.reshape(heads_here, blocks, SPAN).transpose(1, 0, 2)

    steps_fwd = jax.nn.softplus(step_raw[0] + head_params[0, 1][:, None])
    steps_bwd = jax.nn.softplus(step_raw[1] + head_params[1, 1][:, None])[:, ::-1]
    fwd_parts, fwd_end = local_scan(
        ssm_input.reshape(shape_x),
        proj_forward[0].reshape(shape_rows),
        proj_forward[1].reshape(shape_rows),
        to_blocks(steps_fwd),
        head_params[0, 0],
    )
    bwd_parts, bwd_end = local_scan(
        ssm_input[::-1].reshape(shape_x),
        proj_backward[0][::-1].reshape(shape_rows),
        proj_backward[1][::-1].reshape(shape_rows),
        to_blocks(steps_bwd),
        head_params[1, 0],
    )
    decays_all, states_all = tuple(
        (
            part.astype(jnp.float32)
            for part in sent_together(
                (
                    jnp.stack([fwd_end[0], bwd_end[0]])[None].astype(jnp.bfloat16),
                    jnp.stack([fwd_end[1], bwd_end[1]])[None].astype(jnp.bfloat16),
                ),
                "seq",
                0,
                3,
            )
        )
    )
    own_index = lax.axis_index("seq")
    group_size = lax.axis_size("seq")

    def accumulate(position, carried):
        forward_state, backward_state = carried
        mirror = group_size - 1 - position
        forward_state = jnp.where(
            position < own_index,
            decays_all[position, 0][:, None, None] * forward_state + states_all[position, 0],
            forward_state,
        )
        backward_state = jnp.where(
            mirror > own_index,
            decays_all[mirror, 1][:, None, None] * backward_state + states_all[mirror, 1],
            backward_state,
        )
        return (forward_state, backward_state)

    empty_state = jnp.zeros(fwd_end[1].shape, jnp.float32)
    carry_fwd, carry_bwd = lax.fori_loop(0, group_size, accumulate, (empty_state, empty_state))
    forward_out = finish(fwd_parts, carry_fwd)
    backward_out = finish(bwd_parts, carry_bwd)[::-1]
    skipped = (
        ssm_input.reshape(frames, heads_here, width).astype(jnp.float32) * skip_gain[:, None]
    ).reshape(frames, inner_here)
    gated = (forward_out + backward_out + skipped) * jax.nn.silu(gate_z.astype(jnp.float32))
    squares = taken_together(jnp.sum(gated * gated, axis=1), "chan")
    scale = lax.rsqrt(squares / INNER + 1.0)
    normed = (gated * scale[:, None] * norm_gain).astype(jnp.bfloat16)
    frame_share = lax.all_to_all(normed, "chan", split_axis=0, concat_axis=1, tiled=True)
    projected = jnp.dot(
        frame_share,
        lax.all_gather(out_weight, "chan", axis=1, tiled=True),
        preferred_element_type=jnp.float32,
    ).astype(jnp.bfloat16)
    return lax.all_to_all(projected, "chan", split_axis=1, concat_axis=0, tiled=True)


def solution(mesh):
    in_specs = (
        P(("batch", "seq"), "chan"),
        P(("batch", "seq"), "chan"),
        P(None, ("batch", "seq"), None),
        P(None, ("batch", "seq"), None),
        P(None, "chan", ("batch", "seq")),
        P(None, None, "chan"),
        P("chan"),
        P("chan"),
        P(None, "chan"),
    )
    out_specs = P(("batch", "seq"), "chan")
    return jax.shard_map(body, mesh=mesh, in_specs=in_specs, out_specs=out_specs, check_vma=False)
```

profile of v0, /device:TPU:96, one launch (start us, length us, event | category | flops | bytes accessed | tf_op | source)
XLA Modules:
  0.0 171.4 jit_solution(11320585137728651989)
XLA Ops:
  6.5 0.7 all-gather.2.cloned.1.call-update
  7.3 1.2 copy.167
  8.5 6.3 %rev.17 = bf16[1024,256]{1,0:T(8,128)(2,1)S(1)} reverse(bf16[1024,256]{1,0:T(8,128)(2,1)} %param.15), dimensions={0} | reverse | bytes 1048576 | tf_op jit(solution)/shard_map/rev | solution.py:97
  14.9 0.7 slice.57
  15.6 0.8 negate_bitcast_fusion
  16.4 0.8 compare_select_fusion
  17.2 0.7 rev.15
  18.0 4.8 %reduce-window.14 = f32[4,4,2,128]{3,2,1,0:T(2,128)S(1)} reduce-window(f32[4,4,2,128]{3,2,1,0:T(2,128)S(1)} %reshape.296, f32[]{:T(128)} %constant.83.clone.1), window={size=1x1x1x128 pad=0_0x0_0x0_0x127_0}, to_apply=%region_0.1 | reduce-window | flops 520192 | bytes 32772 | tf_op jit(solution)/shard_map/reduce-window
  23.6 1.1 fusion.56
  24.8 1.2 reshape.298
  26.6 1.9 %convolution_bitcast_fusion.3 = f32[4,4,64,128]{3,2,1,0:T(8,128)S(1)} fusion(f32[4,4,256]{2,1,0:T(4,128)S(1)} %get-tuple-element.329, f32[4,256,128]{2,1,0:T(8,128)S(1)} %convert_element_type.76, bf16[4,256,4,64]{1,0,3,2:T(4,128)(2,1)} %reshape.298), kind=kOutput, calls=%fused_computation.48 | convolution fusion | flops 68157440 | bytes 1589248 | tf_op jit(solution)/shard_map/cshp,chsn->chpn/dot_general | solution.py:42
  29.3 4.8 %reduce-window.16 = f32[4,4,2,128]{3,2,1,0:T(2,128)S(1)} reduce-window(f32[4,4,2,128]{3,2,1,0:T(2,128)S(1)} %reshape.300, f32[]{:T(128)} %constant.83.clone.1), window={size=1x1x1x128 pad=0_0x0_0x0_0x127_0}, to_apply=%region_6.7 | reduce-window | flops 520192 | bytes 32772 | tf_op jit(solution)/shard_map/reduce-window.2
  34.9 1.8 %slice_bitcast_fusion = (bf16[1024,128]{1,0:T(8,128)(2,1)}, bf16[1024,128]{1,0:T(8,128)(2,1)S(1)}) fusion(bf16[2,1024,128]{2,1,0:T(8,128)(2,1)} %param.18), kind=kLoop, calls=%fused_computation.70 | loop fusion | bytes 1048576 | tf_op jit(solution)/shard_map/squeeze | solution.py:99
  36.9 0.8 convert_element_type.78
  39.3 2.0 %convolution_bitcast_fusion.2 = f32[4,4,64,128]{3,2,1,0:T(8,128)S(1)} fusion(bf16[4,256,4,64]{1,3,2,0:T(8,128)(2,1)S(1)} %copy.176, f32[4,4,256]{2,1,0:T(4,128)S(1)} %get-tuple-element.324, f32[4,256,128]{2,1,0:T(8,128)} %convert_element_type.78), kind=kOutput, calls=%fused_computation.47 | convolution fusion | flops 68157440 | bytes 1589248 | tf_op jit(solution)/shard_map/cshp,chsn->chpn/dot_general | solution.py:42
  42.7 2.0 %all_gather.6 = bf16[2,2,4,8193]{3,2,1,0:T(4,128)(2,1)S(1)} all-gather(bf16[1,2,4,8193]{3,2,1,0:T(4,128)(2,1)S(1)} %maximum_maximum_fusion), channel_id=1, replica_groups=mesh['seq'=2,'chan'=16,'batch'=8] {'seq'}, dimensions={0}, use_global_device_ids=true | all-gather | bytes 393264 | tf_op jit(solution)/shard_map/all_gather | solution.py:13
  45.4 3.2 %rev.18 = bf16[1024,128]{1,0:T(8,128)(2,1)S(1)} reverse(bf16[1024,128]{1,0:T(8,128)(2,1)} %get-tuple-element.319), dimensions={0} | reverse | bytes 524288 | tf_op jit(solution)/shard_map/rev | solution.py:99
  49.6 3.1 %fusion.22 = f32[4,256,4,64]{1,3,2,0:T(8,128)} fusion(bf16[4,256,4,64]{1,3,2,0:T(8,128)(2,1)S(1)} %copy.176, f32[4,4,256]{2,1,0:T(4,128)} %bitcast.166, f32[4,4,256]{2,1,0:T(4,128)S(1)} %copy-done.9, f32[4,256,256]{2,1,0:T(8,128)S(1)} %fusion.58, pred[256,256]{1,0:T(8,128)(4,1)S(1)} %iota_compare_fusion), kind=kOutput, calls=%fused_computation.37 | convolution fusion | flops 140509184 | bytes 2719744 | tf_op jit(solution)/shard_map/chts,cshp->cthp/dot_general | solution.py:38
  53.0 0.7 copy-done.3
  53.8 1.6 fusion.25
  55.4 0.7 copy.180
  56.3 1.5 rev.19
  58.2 2.5 %fusion.23 = f32[4,256,4,64]{1,3,2,0:T(8,128)S(1)} fusion(f32[4,4,256]{2,1,0:T(4,128)S(1)} %copy-done.13, f32[4,4,256]{2,1,0:T(4,128)S(1)} %copy-done.7, f32[4,256,256]{2,1,0:T(8,128)S(1)} %fusion.57, pred[256,256]{1,0:T(8,128)(4,1)S(1)} %copy-done.11, bf16[4,256,4,64]{1,0,3,2:T(4,128)(2,1)} %reshape.298), kind=kOutput, calls=%fused_computation.38 | convolution fusion | flops 140509184 | bytes 2719744 | tf_op jit(solution)/shard_map/chts,cshp->cthp/dot_general | solution.py:38
  61.1 0.7 copy.178
  61.8 1.2 copy.198
  63.3 1.8 %multiply_reduce_fusion = (f32[1024]{0:T(1024)S(1)}, f32[1024,256]{0,1:T(8,128)S(1)}) fusion(bf16[1024,256]{0,1:T(8,128)(2,1)S(1)} %copy.182, f32[256]{0:T(256)S(1)} %mul.274, bf16[1024,256]{0,1:T(8,128)(2,1)S(1)} %copy.167, f32[1024,256]{0,1:T(8,128)} %bitcast.150, f32[1024,256]{0,1:T(8,128)S(1)} %rev.19), kind=kLoop, calls=%fused_computation.55 | loop fusion | flops 3144704 | bytes 4199424 | tf_op jit(solution)/shard_map/reduce_sum | solution.py:143
  65.2 15.2 %all_to_all.46 = f32[16,1,1024]{2,1,0:T(1,128)S(1)} all-to-all(f32[16,1,1024]{2,1,0:T(1,128)S(1)} %broadcast_in_dim.57), channel_id=1, replica_groups=mesh['seq'=2,'chan'=16,'batch'=8] {'chan'}, dimensions={0} | all-to-all | bytes 131072 | tf_op jit(solution)/shard_map/all_to_all | solution.py:23
  80.8 18.8 %all_to_all.44 = bf16[16,64,256]{2,1,0:T(8,128)(2,1)S(1)} all-to-all(bf16[16,64,256]{2,1,0:T(8,128)(2,1)S(1)} %bitcast.160), channel_id=1, replica_groups=mesh['seq'=2,'chan'=16,'batch'=8] {'chan'}, dimensions={0} | all-to-all | bytes 1048576 | tf_op jit(solution)/shard_map/all_to_all | solution.py:146
  99.7 42.4 %all-gather.2.cloned.1.call-done = bf16[4096,2048]{1,0:T(8,128)(2,1)} async-done(((bf16[4096,128]{1,0:T(8,128)(2,1)}), bf16[4096,2048]{1,0:T(8,128)(2,1)}) %all-gather.2.cloned.1.call-update) | async-done | bytes 16777232 | tf_op jit(solution)/shard_map/all_gather | solution.py:149
  142.1 8.8 %fusion.28 = bf16[8,16,8,128]{3,2,1,0:T(8,128)(2,1)S(1)} fusion(bf16[64,4096]{1,0:T(8,128)(2,1)S(1)} %bitcast.151, bf16[4096,2048]{1,0:T(8,128)(2,1)} %all-gather.2.cloned.1.call-done), kind=kOutput, calls=%fused_computation.49 | convolution fusion | flops 1073872896 | bytes 17563648 | tf_op jit(solution)/shard_map/dot_general | solution.py:147
  150.9 12.9 %all_to_all.45 = bf16[64,16,128]{2,0,1:T(8,128)(2,1)S(1)} all-to-all(bf16[64,16,128]{2,0,1:T(8,128)(2,1)S(1)} %bitcast.162), channel_id=1, replica_groups=mesh['seq'=2,'chan'=16,'batch'=8] {'chan'}, dimensions={1} | all-to-all | bytes 524288 | tf_op jit(solution)/shard_map/all_to_all | solution.py:152
  163.8 0.7 copy.241
  (135 shorter events, 11.0 us)
Async XLA Ops:
  6.5 135.5 %all-gather.2.cloned.1.call-start = ((), (), s32[]{:S(2)}) async-start(), calls=%async_computation.3 | async-start | bytes 17825792 | tf_op jit(solution)/shard_map/all_gather | solution.py:149
  17.9 20.8 %copy-start.5 = (f32[4,1024]{1,0:T(4,128)}, f32[4,1024]{1,0:T(4,128)S(1)}, u32[]{:S(2)}) copy-start(f32[4,1024]{1,0:T(4,128)S(1)} %rev.15) | copy-start | bytes 49156
  18.0 10.6 %copy-start.12 = (f32[4,4,256]{2,1,0:T(4,128)}, f32[4,4,256]{2,1,0:T(4,128)S(1)}, u32[]{:S(2)}) copy-start(f32[4,4,256]{2,1,0:T(4,128)S(1)} %get-tuple-element.314) | copy-start | bytes 49156
  23.3 3.3 %copy-start.6 = (f32[4,4,256]{2,1,0:T(4,128)}, f32[4,4,256]{2,1,0:T(4,128)S(1)}, u32[]{:S(2)}) copy-start(f32[4,4,256]{2,1,0:T(4,128)S(1)} %reduce_window_sum.59) | copy-start | bytes 49156
  29.2 7.5 %copy-start = (f32[4,4,64,128]{3,2,1,0:T(8,128)}, f32[4,4,64,128]{3,2,1,0:T(8,128)S(1)}, u32[]{:S(2)}) copy-start(f32[4,4,64,128]{3,2,1,0:T(8,128)S(1)} %get-tuple-element.216) | copy-start | bytes 1572868
  29.2 7.7 %copy-start.16 = (f32[4,4]{1,0:T(4,128)}, f32[4,4]{1,0:T(4,128)S(1)}, u32[]{:S(2)}) copy-start(f32[4,4]{1,0:T(4,128)S(1)} %get-tuple-element.516) | copy-start | bytes 196
  34.6 6.8 %copy-start.8 = (f32[4,4,256]{2,1,0:T(4,128)}, f32[4,4,256]{2,1,0:T(4,128)S(1)}, u32[]{:S(2)}) copy-start(f32[4,4,256]{2,1,0:T(4,128)S(1)} %reduce_window_sum.62) | copy-start | bytes 49156
  42.0 0.8 copy-start.2
  42.0 7.6 %copy-start.9 = (f32[4,4,256]{2,1,0:T(4,128)S(1)}, f32[4,4,256]{2,1,0:T(4,128)}, u32[]{:S(2)}) copy-start(f32[4,4,256]{2,1,0:T(4,128)} %copy-done.8) | copy-start | bytes 49156
  48.7 4.1 %copy-start.10 = (pred[256,256]{1,0:T(8,128)(4,1)}, pred[256,256]{1,0:T(8,128)(4,1)S(1)}, u32[]{:S(2)}) copy-start(pred[256,256]{1,0:T(8,128)(4,1)S(1)} %iota_compare_fusion) | copy-start | bytes 196612
  52.7 1.0 copy-start.3
  52.7 1.0 copy-start.15
  55.3 2.4 %copy-start.17 = (f32[4,4]{1,0:T(4,128)S(1)}, f32[4,4]{1,0:T(4,128)}, u32[]{:S(2)}) copy-start(f32[4,4]{1,0:T(4,128)} %copy-done.16) | copy-start | bytes 196
  55.3 2.8 %copy-start.7 = (f32[4,4,256]{2,1,0:T(4,128)S(1)}, f32[4,4,256]{2,1,0:T(4,128)}, u32[]{:S(2)}) copy-start(f32[4,4,256]{2,1,0:T(4,128)} %copy-done.6) | copy-start | bytes 49156
  55.4 2.8 %copy-start.11 = (pred[256,256]{1,0:T(8,128)(4,1)S(1)}, pred[256,256]{1,0:T(8,128)(4,1)}, u32[]{:S(2)}) copy-start(pred[256,256]{1,0:T(8,128)(4,1)} %copy-done.10) | copy-start | bytes 196612
  55.4 2.8 %copy-start.13 = (f32[4,4,256]{2,1,0:T(4,128)S(1)}, f32[4,4,256]{2,1,0:T(4,128)}, u32[]{:S(2)}) copy-start(f32[4,4,256]{2,1,0:T(4,128)} %copy-done.12) | copy-start | bytes 49156
  58.2 2.5 %copy-start.1 = (f32[4,4,64,128]{3,2,1,0:T(8,128)S(1)}, f32[4,4,64,128]{3,2,1,0:T(8,128)}, u32[]{:S(2)}) copy-start(f32[4,4,64,128]{3,2,1,0:T(8,128)} %copy-done) | copy-start | bytes 1572868
  58.2 2.5 %copy-start.14 = (f32[4,256,4]{1,2,0:T(4,128)S(1)}, f32[4,256,4]{1,2,0:T(4,128)}, u32[]{:S(2)}) copy-start(f32[4,256,4]{1,2,0:T(4,128)} %get-tuple-element.330) | copy-start | bytes 49156
  60.7 2.3 %copy-start.4 = (bf16[1024,256]{1,0:T(8,128)(2,1)S(1)}, bf16[1024,256]{1,0:T(8,128)(2,1)}, u32[]{:S(2)}) copy-start(bf16[1024,256]{1,0:T(8,128)(2,1)} %param.16) | copy-start | bytes 1572868
  60.7 2.5 %copy-start.19 = (f32[4]{0:T(128)S(1)}, f32[4]{0:T(128)}, u32[]{:S(2)}) copy-start(f32[4]{0:T(128)} %param.21) | copy-start | bytes 52
  61.8 18.7 %copy-start.18 = (f32[256]{0:T(256)S(1)}, f32[256]{0:T(256)}, u32[]{:S(2)}) copy-start(f32[256]{0:T(256)} %param.22) | copy-start | bytes 3076
Sparse Core Ops, SparseCore 0:
  9.7 132.2 all-gather.1
where the time goes:
time: 173 us; the launch traced here: 171 us
  blocking collectives  48.9 us (28%)
  waiting for transfers between devices  43.1 us (25%)
  local copies, waits for them, and re-layouts  26 us (15%)
  matrix products  20.8 us (12%)
  other arithmetic  18.2 us (11%)
  between operations  14 us (8%)
    all_gather x1, waiting for transfers between devices, body(): lax.all_gather(out_weight, 'chan', axis=1, tiled=True)  42.4 us
    all_to_all x1, blocking collectives, body(): lax.all_to_all(normed, 'chan', split_axis=0, concat_axis=1, tiled=True)  18.8 us
    all_to_all x1, blocking collectives, copy_for_each(): return lax.all_to_all(copies, axis, split_axis=0, concat_axis=0, tiled=True)  15.2 us
    all_to_all x1, blocking collectives, body(): lax.all_to_all(projected, 'chan', split_axis=1, concat_axis=0, tiled=True)  12.9 us
    another operation x8, other arithmetic  9.88 us
    dot_general x1, matrix products, body(): jnp.dot(frame_share, lax.all_gather(out_weight, 'chan', axis=1, tiled=Tru...  8.79 us
    rev x1, local copies, waits for them, and re-layouts, body(): ssm_input[::-1].reshape(shape_x)  6.33 us
    dot_general x2, matrix products, local_scan(): jnp.einsum('chts,cshp->cthp', weights, blocks_x, preferred_element_type=j...  5.62 us
  transfers between devices with their start and end apart: 1, of which 1 were waited for; matrix products, arithmetic and copies ran while one was open for 32% of the time, Pallas kernels for 0%

commit v1 on v0

--- a/solution.py
+++ b/solution.py
@@ -149,7 +149,12 @@
         lax.all_gather(out_weight, "chan", axis=1, tiled=True),
         preferred_element_type=jnp.float32,
     ).astype(jnp.bfloat16)
-    return lax.all_to_all(projected, "chan", split_axis=1, concat_axis=0, tiled=True)
+    return jnp.concatenate(
+        lax.all_to_all(
+            jnp.stack(jnp.split(projected, lax.axis_size("chan"), axis=1)), "chan", 0, 0
+        ),
+        axis=0,
+    )
 
 
 def solution(mesh):

time: 173 us -> 174 us (level)
    all_to_all x1, blocking collectives: 18.8 us -> 17 us  [body(): lax.all_to_all(normed, 'chan', split_axis=0, concat_axis=1, tiled=True)]
    unnamed x47 -> x54, local copies, waits for them, and re-layouts: 4.97 us -> 5.2 us
  transfers between devices with their start and end apart: 1 -> 1, of which waited for: 1 -> 1; matrix products, arithmetic and copies ran while one was open for 32% -> 31% of each run, Pallas kernels for 0% -> 0%
where the time goes in v1:
time: 174 us; the launch traced here: 171 us
  blocking collectives  47.4 us (27%)
  waiting for transfers between devices  44.5 us (26%)
  local copies, waits for them, and re-layouts  26.2 us (15%)
  matrix products  20.8 us (12%)
  other arithmetic  17.6 us (10%)
  between operations  14 us (8%)
    all_gather x1, waiting for transfers between devices, body(): lax.all_gather(out_weight, 'chan', axis=1, tiled=True)  43.8 us
    all_to_all x1, blocking collectives, body(): lax.all_to_all(normed, 'chan', split_axis=0, concat_axis=1, tiled=True)  17 us
    all_to_all x1, blocking collectives, copy_for_each(): return lax.all_to_all(copies, axis, split_axis=0, concat_axis=0, tiled=True)  15.2 us
    all_to_all x1, blocking collectives, body(): lax.all_to_all(jnp.stack(jnp.split(projected, lax.axis_size('chan'), axis...  13.3 us
    another operation x8, other arithmetic  9.88 us
    dot_general x1, matrix products, body(): jnp.dot(frame_share, lax.all_gather(out_weight, 'chan', axis=1, tiled=Tru...  8.79 us
    rev x1, local copies, waits for them, and re-layouts, body(): ssm_input[::-1].reshape(shape_x)  6.33 us
    dot_general x2, matrix products, local_scan(): jnp.einsum('chts,cshp->cthp', weights, blocks_x, preferred_element_type=j...  5.64 us
  transfers between devices with their start and end apart: 1, of which 1 were waited for; matrix products, arithmetic and copies ran while one was open for 31% of the time, Pallas kernels for 0%

profile of v1, /device:TPU:96, one launch (start us, length us, event | category | flops | bytes accessed | tf_op | source)
XLA Modules:
  0.0 171.0 jit_solution(10512512988679347163)
XLA Ops:
  6.5 0.7 all-gather.2.cloned.1.call-update
  7.3 1.2 copy.160
  8.5 6.3 %rev.17 = bf16[1024,256]{1,0:T(8,128)(2,1)S(1)} reverse(bf16[1024,256]{1,0:T(8,128)(2,1)} %param.15), dimensions={0} | reverse | bytes 1048576 | tf_op jit(solution)/shard_map/rev | solution.py:97
  14.9 0.7 slice.57
  15.6 0.8 negate_bitcast_fusion
  16.4 0.8 compare_select_fusion
  17.2 0.7 rev.15
  18.0 4.8 %reduce-window.14 = f32[4,4,2,128]{3,2,1,0:T(2,128)S(1)} reduce-window(f32[4,4,2,128]{3,2,1,0:T(2,128)S(1)} %reshape.296, f32[]{:T(128)} %constant.83.clone.1), window={size=1x1x1x128 pad=0_0x0_0x0_0x127_0}, to_apply=%region_0.1 | reduce-window | flops 520192 | bytes 32772 | tf_op jit(solution)/shard_map/reduce-window
  23.6 1.1 fusion.55
  24.8 1.2 reshape.298
  26.6 1.9 %convolution_bitcast_fusion.3 = f32[4,4,64,128]{3,2,1,0:T(8,128)S(1)} fusion(f32[4,4,256]{2,1,0:T(4,128)S(1)} %get-tuple-element.329, f32[4,256,128]{2,1,0:T(8,128)S(1)} %convert_element_type.76, bf16[4,256,4,64]{1,0,3,2:T(4,128)(2,1)} %reshape.298), kind=kOutput, calls=%fused_computation.48 | convolution fusion | flops 68157440 | bytes 1589248 | tf_op jit(solution)/shard_map/cshp,chsn->chpn/dot_general | solution.py:42
  29.2 4.8 %reduce-window.16 = f32[4,4,2,128]{3,2,1,0:T(2,128)S(1)} reduce-window(f32[4,4,2,128]{3,2,1,0:T(2,128)S(1)} %reshape.300, f32[]{:T(128)} %constant.83.clone.1), window={size=1x1x1x128 pad=0_0x0_0x0_0x127_0}, to_apply=%region_6.7 | reduce-window | flops 520192 | bytes 32772 | tf_op jit(solution)/shard_map/reduce-window.2
  34.8 1.8 %slice_bitcast_fusion = (bf16[1024,128]{1,0:T(8,128)(2,1)}, bf16[1024,128]{1,0:T(8,128)(2,1)S(1)}) fusion(bf16[2,1024,128]{2,1,0:T(8,128)(2,1)} %param.18), kind=kLoop, calls=%fused_computation.68 | loop fusion | bytes 1048576 | tf_op jit(solution)/shard_map/squeeze | solution.py:99
  36.9 0.8 convert_element_type.78
  39.3 2.0 %convolution_bitcast_fusion.2 = f32[4,4,64,128]{3,2,1,0:T(8,128)S(1)} fusion(bf16[4,256,4,64]{1,3,2,0:T(8,128)(2,1)S(1)} %copy.169, f32[4,4,256]{2,1,0:T(4,128)S(1)} %get-tuple-element.324, f32[4,256,128]{2,1,0:T(8,128)} %convert_element_type.78), kind=kOutput, calls=%fused_computation.47 | convolution fusion | flops 68157440 | bytes 1589248 | tf_op jit(solution)/shard_map/cshp,chsn->chpn/dot_general | solution.py:42
  42.7 2.0 %all_gather.6 = bf16[2,2,4,8193]{3,2,1,0:T(4,128)(2,1)S(1)} all-gather(bf16[1,2,4,8193]{3,2,1,0:T(4,128)(2,1)S(1)} %maximum_maximum_fusion), channel_id=1, replica_groups=mesh['seq'=2,'chan'=16,'batch'=8] {'seq'}, dimensions={0}, use_global_device_ids=true | all-gather | bytes 393264 | tf_op jit(solution)/shard_map/all_gather | solution.py:13
  45.3 3.2 %rev.18 = bf16[1024,128]{1,0:T(8,128)(2,1)S(1)} reverse(bf16[1024,128]{1,0:T(8,128)(2,1)} %get-tuple-element.319), dimensions={0} | reverse | bytes 524288 | tf_op jit(solution)/shard_map/rev | solution.py:99
  48.9 3.1 %fusion.22 = f32[4,256,4,64]{1,3,2,0:T(8,128)} fusion(bf16[4,256,4,64]{1,3,2,0:T(8,128)(2,1)S(1)} %copy.169, f32[4,4,256]{2,1,0:T(4,128)} %bitcast.222, f32[4,4,256]{2,1,0:T(4,128)S(1)} %copy-done.9, f32[4,256,256]{2,1,0:T(8,128)S(1)} %fusion.57, pred[256,256]{1,0:T(8,128)(4,1)S(1)} %iota_compare_fusion), kind=kOutput, calls=%fused_computation.37 | convolution fusion | flops 140509184 | bytes 2719744 | tf_op jit(solution)/shard_map/chts,cshp->cthp/dot_general | solution.py:38
  52.4 0.7 copy-done.3
  53.1 1.6 fusion.25
  54.7 0.7 copy.173
  55.6 1.5 rev.19
  57.5 2.5 %fusion.23 = f32[4,256,4,64]{1,3,2,0:T(8,128)S(1)} fusion(f32[4,4,256]{2,1,0:T(4,128)S(1)} %copy-done.11, f32[4,4,256]{2,1,0:T(4,128)S(1)} %copy-done.7, f32[4,256,256]{2,1,0:T(8,128)S(1)} %fusion.56, pred[256,256]{1,0:T(8,128)(4,1)S(1)} %iota_compare_fusion, bf16[4,256,4,64]{1,0,3,2:T(4,128)(2,1)} %reshape.298), kind=kOutput, calls=%fused_computation.38 | convolution fusion | flops 140509184 | bytes 2719744 | tf_op jit(solution)/shard_map/chts,cshp->cthp/dot_general | solution.py:38
  60.4 0.7 copy.171
  61.1 1.2 copy.189
  62.7 1.8 %multiply_reduce_fusion = (f32[1024]{0:T(1024)S(1)}, f32[1024,256]{0,1:T(8,128)S(1)}) fusion(bf16[1024,256]{0,1:T(8,128)(2,1)S(1)} %copy.175, f32[256]{0:T(256)S(1)} %mul.274, bf16[1024,256]{0,1:T(8,128)(2,1)S(1)} %copy.160, f32[1024,256]{0,1:T(8,128)} %bitcast.207, f32[1024,256]{0,1:T(8,128)S(1)} %rev.19), kind=kLoop, calls=%fused_computation.54 | loop fusion | flops 3144704 | bytes 4199424 | tf_op jit(solution)/shard_map/reduce_sum | solution.py:143
  64.6 15.2 %all_to_all.32 = f32[16,1,1024]{2,1,0:T(1,128)S(1)} all-to-all(f32[16,1,1024]{2,1,0:T(1,128)S(1)} %broadcast_in_dim.57), channel_id=1, replica_groups=mesh['seq'=2,'chan'=16,'batch'=8] {'chan'}, dimensions={0} | all-to-all | bytes 131072 | tf_op jit(solution)/shard_map/all_to_all | solution.py:23
  80.2 17.0 %all_to_all.30 = bf16[16,64,256]{2,1,0:T(8,128)(2,1)S(1)} all-to-all(bf16[16,64,256]{2,1,0:T(8,128)(2,1)S(1)} %bitcast.217), channel_id=1, replica_groups=mesh['seq'=2,'chan'=16,'batch'=8] {'chan'}, dimensions={0} | all-to-all | bytes 1048576 | tf_op jit(solution)/shard_map/all_to_all | solution.py:146
  97.2 43.8 %all-gather.2.cloned.1.call-done = bf16[4096,2048]{1,0:T(8,128)(2,1)} async-done(((bf16[4096,128]{1,0:T(8,128)(2,1)}), bf16[4096,2048]{1,0:T(8,128)(2,1)}) %all-gather.2.cloned.1.call-update) | async-done | bytes 16777232 | tf_op jit(solution)/shard_map/all_gather | solution.py:149
  141.0 8.8 %convolution_convert_fusion = bf16[64,2048]{1,0:T(8,128)(2,1)S(1)} fusion(bf16[64,4096]{1,0:T(8,128)(2,1)S(1)} %bitcast.208, bf16[4096,2048]{1,0:T(8,128)(2,1)} %all-gather.2.cloned.1.call-done), kind=kOutput, calls=%fused_computation.20 | convolution fusion | flops 1073872896 | bytes 17563648 | tf_op jit(solution)/shard_map/dot_general | solution.py:147
  150.1 13.3 %all_to_all.31 = bf16[16,64,128]{2,1,0:T(8,128)(2,1)S(1)} all-to-all(bf16[16,64,128]{2,1,0:T(8,128)(2,1)S(1)} %constant_dynamic-update-slice_fusion), channel_id=1, replica_groups=mesh['seq'=2,'chan'=16,'batch'=8] {'chan'}, dimensions={0} | all-to-all | bytes 524288 | tf_op jit(solution)/shard_map/all_to_all | solution.py:153
  163.4 0.7 copy.245
  (142 shorter events, 10.5 us)
Async XLA Ops:
  6.5 134.5 %all-gather.2.cloned.1.call-start = ((), (), s32[]{:S(2)}) async-start(), calls=%async_computation.3 | async-start | bytes 17825792 | tf_op jit(solution)/shard_map/all_gather | solution.py:149
  17.9 20.8 %copy-start.5 = (f32[4,1024]{1,0:T(4,128)}, f32[4,1024]{1,0:T(4,128)S(1)}, u32[]{:S(2)}) copy-start(f32[4,1024]{1,0:T(4,128)S(1)} %rev.15) | copy-start | bytes 49156
  18.0 10.6 %copy-start.10 = (f32[4,4,256]{2,1,0:T(4,128)}, f32[4,4,256]{2,1,0:T(4,128)S(1)}, u32[]{:S(2)}) copy-start(f32[4,4,256]{2,1,0:T(4,128)S(1)} %get-tuple-element.314) | copy-start | bytes 49156
  23.3 3.3 %copy-start.6 = (f32[4,4,256]{2,1,0:T(4,128)}, f32[4,4,256]{2,1,0:T(4,128)S(1)}, u32[]{:S(2)}) copy-start(f32[4,4,256]{2,1,0:T(4,128)S(1)} %reduce_window_sum.59) | copy-start | bytes 49156
  29.2 7.5 %copy-start = (f32[4,4,64,128]{3,2,1,0:T(8,128)}, f32[4,4,64,128]{3,2,1,0:T(8,128)S(1)}, u32[]{:S(2)}) copy-start(f32[4,4,64,128]{3,2,1,0:T(8,128)S(1)} %get-tuple-element.216) | copy-start | bytes 1572868
  34.5 6.8 %copy-start.8 = (f32[4,4,256]{2,1,0:T(4,128)}, f32[4,4,256]{2,1,0:T(4,128)S(1)}, u32[]{:S(2)}) copy-start(f32[4,4,256]{2,1,0:T(4,128)S(1)} %reduce_window_sum.62) | copy-start | bytes 49156
  41.9 0.8 copy-start.2
  41.9 7.0 %copy-start.9 = (f32[4,4,256]{2,1,0:T(4,128)S(1)}, f32[4,4,256]{2,1,0:T(4,128)}, u32[]{:S(2)}) copy-start(f32[4,4,256]{2,1,0:T(4,128)} %copy-done.8) | copy-start | bytes 49156
  52.1 1.0 copy-start.3
  52.1 1.0 copy-start.13
  54.7 2.8 %copy-start.7 = (f32[4,4,256]{2,1,0:T(4,128)S(1)}, f32[4,4,256]{2,1,0:T(4,128)}, u32[]{:S(2)}) copy-start(f32[4,4,256]{2,1,0:T(4,128)} %copy-done.6) | copy-start | bytes 49156
  54.7 2.8 %copy-start.11 = (f32[4,4,256]{2,1,0:T(4,128)S(1)}, f32[4,4,256]{2,1,0:T(4,128)}, u32[]{:S(2)}) copy-start(f32[4,4,256]{2,1,0:T(4,128)} %copy-done.10) | copy-start | bytes 49156
  57.5 2.5 %copy-start.1 = (f32[4,4,64,128]{3,2,1,0:T(8,128)S(1)}, f32[4,4,64,128]{3,2,1,0:T(8,128)}, u32[]{:S(2)}) copy-start(f32[4,4,64,128]{3,2,1,0:T(8,128)} %copy-done) | copy-start | bytes 1572868
  57.5 2.5 %copy-start.12 = (f32[4,256,4]{1,2,0:T(4,128)S(1)}, f32[4,256,4]{1,2,0:T(4,128)}, u32[]{:S(2)}) copy-start(f32[4,256,4]{1,2,0:T(4,128)} %get-tuple-element.330) | copy-start | bytes 49156
  60.0 2.3 %copy-start.4 = (bf16[1024,256]{1,0:T(8,128)(2,1)S(1)}, bf16[1024,256]{1,0:T(8,128)(2,1)}, u32[]{:S(2)}) copy-start(bf16[1024,256]{1,0:T(8,128)(2,1)} %param.16) | copy-start | bytes 1572868
  60.0 2.5 %copy-start.15 = (f32[4]{0:T(128)S(1)}, f32[4]{0:T(128)}, u32[]{:S(2)}) copy-start(f32[4]{0:T(128)} %param.21) | copy-start | bytes 52
  61.1 18.7 %copy-start.14 = (f32[256]{0:T(256)S(1)}, f32[256]{0:T(256)}, u32[]{:S(2)}) copy-start(f32[256]{0:T(256)} %param.22) | copy-start | bytes 3076
Sparse Core Ops, SparseCore 0:
  9.7 131.2 all-gather.1
